TPU v7x, 32 devices: a whole 2x2x4 slice. The times are simulated.
32 devices in a mesh: track: 4 (over y, x), ifg: 4 (over z), pix: 2 (over core).
Axes of the slice: x: 2, y: 2, z: 4, core: 2. Of those that a mesh axis runs over, the one named last changes fastest.
Arguments:
- phases: bfloat16 [4, 600, 32768], P('track', 'ifg', 'pix')
- pairs: int32 [4, 600, 2], P('track', 'ifg'), may hold values from 0 to 249, as said below
- date_map: int32 [4, 250], replicated, may hold values from 0 to 319, as said below
- knots: int32 [32], replicated, may hold values from 0 to 319, as said below
- look: float32 [4, 3, 32768], P(None, None, 'pix'), may hold values from -1 to 1
Outputs:
- enu: float32 [3, 320, 32768], P(None, None, ('pix', 'ifg', 'track'))
- spline: float32 [3, 32, 32768], P(None, None, ('pix', 'ifg', 'track'))
Inputs may be any that keep to these rules, and one draw needn't show every extreme that they name: pairs[t, k, 0] < pairs[t, k, 1] <= pairs[t, k, 0] + 5. `date_map`: the dates of one track map to distinct epochs. `knots`: strictly increasing, the first 0 and the last 319.
All inputs are finite; a program needn't handle non-finite values.
Results may differ from a plain program's by a relative error of at most 0.0003.
Values may be sent and summed in bfloat16 or wider, within the bound.
A program may use at most 128 MiB of HBM per device.

v0:
```python
import jax
import jax.numpy as jnp
from jax import lax
from jax.sharding import PartitionSpec as P

EPOCHS = 320
damping = 0.5
ridge = 0.1
HIGH = lax.Precision.HIGHEST


def incidence(pair_rows, ndate):
    dates = jnp.arange(ndate, dtype=jnp.int32)[:, None]
    later = (dates == pair_rows[None, :, 1]).astype(jnp.float32)
    earlier = (dates == pair_rows[None, :, 0]).astype(jnp.float32)
    return later - earlier


def inverse_normal(normal_part):
    ndate = normal_part.shape[0]
    normal = normal_part + damping * jnp.eye(ndate, dtype=jnp.float32)
    factor = jnp.linalg.cholesky(normal)
    return jax.scipy.linalg.cho_solve((factor, True), jnp.eye(ndate, dtype=jnp.float32))


def hat_basis(knots, n_epochs):
    spots = knots.astype(jnp.float32)
    left = jnp.concatenate([spots[:1] - 1.0, spots[:-1]])
    right = jnp.concatenate([spots[1:], spots[-1:] + 1.0])
    epochs = jnp.arange(n_epochs, dtype=jnp.float32)[:, None]
    rise = (epochs - left) / (spots - left)
    fall = (right - epochs) / (right - spots)
    return jnp.maximum(0.0, jnp.minimum(rise, fall))


def geometry(series, date_map, look, knots, n_epochs):
    epochs = jnp.arange(n_epochs, dtype=jnp.int32)
    onehot = (date_map[:, None, :] == epochs[None, :, None]).astype(jnp.float32)
    seen = jnp.sum(onehot, axis=2)
    resampled = jnp.einsum("tcd,tdp->tcp", onehot, series, precision=HIGH)

    def entry(first, second):
        value = jnp.einsum("tc,tp->cp", seen, look[:, first] * look[:, second], precision=HIGH)
        if first == second:
            value = value + ridge
        return value

    a00, a01, a02 = (entry(0, 0), entry(0, 1), entry(0, 2))
    a11, a12, a22 = (entry(1, 1), entry(1, 2), entry(2, 2))
    b_all = [jnp.sum(look[:, i][:, None, :] * resampled, axis=0) for i in range(3)]
    c00 = a11 * a22 - a12 * a12
    c01 = a02 * a12 - a01 * a22
    c02 = a01 * a12 - a02 * a11
    c11 = a00 * a22 - a02 * a02
    c12 = a01 * a02 - a00 * a12
    c22 = a00 * a11 - a01 * a01
    det = a00 * c00 + a01 * c01 + a02 * c02
    east = (c00 * b_all[0] + c01 * b_all[1] + c02 * b_all[2]) / det
    north = (c01 * b_all[0] + c11 * b_all[1] + c12 * b_all[2]) / det
    upward = (c02 * b_all[0] + c12 * b_all[1] + c22 * b_all[2]) / det
    enu = jnp.stack([east, north, upward])
    basis = hat_basis(knots, n_epochs)
    gram = jnp.dot(basis.T, basis, precision=HIGH)
    factor = jnp.linalg.cholesky(gram)
    fitter = jax.scipy.linalg.cho_solve((factor, True), basis.T)
    spline = jnp.einsum("kc,icp->ikp", fitter, enu, precision=HIGH)
    return (enu, spline)


def shards(phases, pairs, date_map, knots, look):
    ndate = date_map.shape[1]
    n_epochs = hat_count()
    n_track = lax.axis_size("track")
    n_ifg = lax.axis_size("ifg")
    width = phases.shape[2] // (n_track * n_ifg)
    offset = lax.axis_index("ifg") * (width * n_track) + lax.axis_index("track") * width
    look_local = lax.dynamic_slice_in_dim(look, offset, width, 2)
    phase_rows = phases[0]
    pair_rows = pairs[0]
    phase_all = lax.all_to_all(phase_rows, "ifg", split_axis=1, concat_axis=0, tiled=True)
    pair_all = lax.all_gather(pair_rows, "ifg", axis=0, tiled=True)
    incid = incidence(pair_all, ndate)
    normal_part = jnp.dot(incid, incid.T, precision=HIGH)
    rhs = jnp.dot(incid.astype(jnp.bfloat16), phase_all, preferred_element_type=jnp.float32)
    ninv = inverse_normal(normal_part)
    pixel_count = rhs.shape[1] * lax.axis_size("ifg") * lax.axis_size("pix")
    series = jnp.dot(ninv, rhs, precision=HIGH)
    total = lax.psum(jnp.sum(series, axis=1), ("ifg", "pix"))
    series = series - (total / pixel_count)[:, None]
    gathered = lax.all_to_all(series[None], "track", split_axis=2, concat_axis=0, tiled=True)
    return geometry(gathered, date_map, look_local, knots, n_epochs)


def hat_count():
    return EPOCHS


def solution(mesh):
    in_specs = (P("track", "ifg", "pix"), P("track", "ifg", None), P(), P(), P(None, None, "pix"))
    out_specs = (P(None, None, ("pix", "ifg", "track")), P(None, None, ("pix", "ifg", "track")))
    return jax.shard_map(shards, mesh=mesh, in_specs=in_specs, out_specs=out_specs, check_vma=False)
```

profile of v0, /device:TPU:0, one launch (start us, length us, event | category | flops | bytes accessed | tf_op | source)
XLA Modules:
  0.0 324.4 jit_solution(3422282366233087118)
XLA Ops:
  0.6 11.1 %all_to_all.27 = bf16[150,4,4096]{2,1,0:T(4,128)(2,1)} reshape(bf16[1,150,16384]{2,1,0:T(8,128)(2,1)} %param.5) | data formatting | bytes 9830400 | tf_op jit(solution)/shard_map/all_to_all | solution.py:80
  11.7 7.3 %copy.23 = bf16[150,4,4096]{2,0,1:T(8,128)(2,1)} copy(bf16[150,4,4096]{2,1,0:T(4,128)(2,1)} %all_to_all.27) | data formatting | bytes 9830400 | tf_op jit(solution)/shard_map/all_to_all | solution.py:80
  19.1 6.5 %all-to-all-start = ((bf16[150,4,4096]{2,0,1:T(8,128)(2,1)}), bf16[150,4,4096]{2,0,1:T(8,128)(2,1)}, u32[]{:S(2)}, u32[]{:S(2)}) async-start(bf16[150,4,4096]{2,0,1:T(8,128)(2,1)} %copy.23), calls=%async_computation | async-start | bytes 9961472 | tf_op jit(solution)/shard_map/all_to_all | solution.py:80
  25.7 118.2 %all-gather = s32[1,600,2]{2,0,1:T(1,128)S(1)} all-gather(s32[1,150,2]{2,0,1:T(1,128)S(1)} %copy.21), channel_id=2, replica_groups=mesh['track'=4,'ifg'=4,'pix'=2] {'ifg'}, dimensions={1}, use_global_device_ids=true | all-gather | bytes 6000 | tf_op jit(solution)/shard_map/all_gather | solution.py:81
  144.3 1.0 fusion.3
  145.5 11.7 %cholesky.63 = f32[128,128]{1,0:T(8,128)S(1)} custom-call(f32[128,128]{1,0:T(8,128)S(1)} %cholesky.156), custom_call_target="Cholesky" | custom-call | tf_op jit(solution)/shard_map/jit(cholesky)/cholesky | solution.py:22
  157.3 9.8 %custom-call.28 = f32[1,128,128]{1,2,0:T(8,128)S(1)} custom-call(f32[1,128,128]{2,1,0:T(8,128)S(1)} %get-tuple-element.40), custom_call_target="InvertDiagBlocksLowerTriangular" | custom-call | tf_op jit(solution)/shard_map/jit(cholesky)/cholesky | solution.py:22
  167.6 11.2 %cholesky.133 = f32[122,122]{1,0:T(8,128)S(1)} custom-call(f32[122,122]{1,0:T(8,128)S(1)} %convolution_subtract_fusion.2), custom_call_target="Cholesky" | custom-call | tf_op jit(solution)/shard_map/jit(cholesky)/cholesky | solution.py:22
  181.6 20.2 %custom-call.29 = f32[2,128,128]{1,2,0:T(8,128)S(1)} custom-call(f32[2,128,128]{2,1,0:T(8,128)S(1)} %pad_maximum_fusion.1), custom_call_target="InvertDiagBlocksLowerTriangular" | custom-call | tf_op jit(solution)/shard_map/jit(_cho_solve)/triangular_solve | solution.py:23
  203.6 6.0 %all_to_all.30 = bf16[600,4096]{1,0:T(8,128)(2,1)} reshape(bf16[4,150,4096]{2,1,0:T(8,128)(2,1)} %bitcast.11) | data formatting | bytes 9830400 | tf_op jit(solution)/shard_map/all_to_all | solution.py:80
  209.6 4.2 %fusion.5 = f32[250,4096]{1,0:T(8,128)S(1)} fusion(bf16[600,4096]{1,0:T(8,128)(2,1)} %all_to_all.30, s32[600]{0:T(1024)S(1)} %get-tuple-element.26, s32[600]{0:T(1024)S(1)} %get-tuple-element.25), kind=kOutput, calls=%fused_computation.31 | convolution fusion | flops 1229699968 | bytes 9016000 | tf_op jit(solution)/shard_map/dot_general | solution.py:84
  213.8 5.3 %fusion.48 = (f32[250]{0:T(256)S(1)}, f32[250,4096]{1,0:T(8,128)}) fusion(f32[250,4096]{1,0:T(8,128)S(1)} %fusion.5, f32[122,250]{1,0:T(8,128)S(1)} %fusion.26, f32[128,250]{1,0:T(8,128)S(1)} %fusion.25), kind=kOutput, calls=%fused_computation.113 | convolution fusion | flops 3073086208 | bytes 8443000 | tf_op jit(solution)/shard_map/dot_general | solution.py:87
  219.1 13.6 %psum.7 = f32[250]{0:T(256)S(1)} all-reduce(f32[250]{0:T(256)S(1)} %get-tuple-element.49), channel_id=1, replica_groups=mesh['track'=4,'ifg'=4,'pix'=2] {'ifg','pix'}, use_global_device_ids=true, to_apply=%region_6.7 | all-reduce | flops 250 | bytes 2000 | tf_op jit(solution)/shard_map/psum | solution.py:88
  232.7 4.7 %subtract_bitcast_fusion = f32[1,250,4096]{2,1,0:T(8,128)} fusion(f32[250,4096]{1,0:T(8,128)} %get-tuple-element.50, f32[250]{0:T(256)S(1)} %broadcast_multiply_fusion), kind=kLoop, calls=%fused_computation.5 | loop fusion | flops 1024000 | bytes 8193000 | tf_op jit(solution)/shard_map/broadcast_in_dim | solution.py:90
  237.4 10.2 %copy.24 = f32[1,250,4096]{1,0,2:T(1,128)} copy(f32[1,250,4096]{2,1,0:T(8,128)} %subtract_bitcast_fusion) | data formatting | bytes 8192000 | tf_op jit(solution)/shard_map/broadcast_in_dim | solution.py:90
  247.6 5.0 %all-to-all-start.1 = ((f32[1,250,4096]{1,0,2:T(1,128)}), f32[1,250,4096]{1,0,2:T(1,128)}, u32[]{:S(2)}, u32[]{:S(2)}) async-start(f32[1,250,4096]{1,0,2:T(1,128)} %copy.24), calls=%async_computation.1 | async-start | bytes 8388608 | tf_op jit(solution)/shard_map/all_to_all | solution.py:90
  255.1 2.9 cholesky.147
  258.1 0.6 compare_reduce_fusion
  258.7 0.7 fusion.30
  259.4 2.4 custom-call.30
  261.8 0.8 dynamic-slice_bitcast_fusion.2
  263.5 2.4 convolution_add_fusion
  265.8 2.4 convolution_add_fusion.1
  268.2 2.3 convolution_add_fusion.2
  270.5 1.2 fusion.35
  271.8 1.3 fusion.37
  273.0 27.3 %all-to-all-done.1 = f32[1,250,4096]{1,0,2:T(1,128)} async-done(((f32[1,250,4096]{1,0,2:T(1,128)}), f32[1,250,4096]{1,0,2:T(1,128)}, u32[]{:S(2)}, u32[]{:S(2)}) %all-to-all-start.1) | async-done | bytes 4096032 | tf_op jit(solution)/shard_map/all_to_all | solution.py:90
  300.3 4.4 %copy.27 = f32[1,250,4096]{1,2,0:T(8,128)} copy(f32[1,250,4096]{1,0,2:T(1,128)} %all-to-all-done.1) | data formatting | bytes 8192000
  304.8 5.6 %copy.25 = f32[1,250,4,1024]{3,1,2,0:T(8,128)} copy(f32[1,250,4,1024]{1,3,2,0:T(8,128)} %bitcast.82) | data formatting | bytes 8192000 | tf_op jit(solution)/shard_map/all_to_all | solution.py:90
  310.4 6.9 %multiply_reduce_fusion.2 = (f32[320,1024]{1,0:T(8,128)S(1)}, f32[320,1024]{1,0:T(8,128)S(1)}, f32[320,1024]{1,0:T(8,128)S(1)}) fusion(f32[4,1024]{1,0:T(4,128)S(1)} %get-tuple-element.36, f32[4,1024]{1,0:T(4,128)S(1)} %get-tuple-element.35, f32[4,1024]{1,0:T(4,128)S(1)} %get-tuple-element.34, f32[1,250,4,1024]{3,1,2,0:T(8,128)} %copy.25, ...), kind=kOutput, calls=%fused_computation.2 | convolution fusion | flops 3939361280 | bytes 8081312 | tf_op jit(solution)/shard_map/tcd,tdp->tcp/dot_general | solution.py:40
  317.3 3.0 divide_bitcast_fusion.2
  320.9 3.3 %convolution_bitcast_fusion = f32[3,32,1024]{2,1,0:T(8,128)} fusion(f32[3,320,1024]{2,1,0:T(8,128)S(1)} %pad_maximum_fusion, f32[32,320,1]{1,0,2:T(8,128)S(1)} %convolution_bitcast_fusion.1), kind=kOutput, calls=%fused_computation.20 | convolution fusion | flops 377487360 | bytes 4366336 | tf_op jit(solution)/shard_map/kc,icp->ikp/dot_general | solution.py:66
  (53 shorter events, 7.0 us)
Async XLA Ops:
  19.1 6.5 %copy-start.5 = (s32[1,150,2]{1,2,0:T(2,128)S(1)}, s32[1,150,2]{1,2,0:T(2,128)}, u32[]{:S(2)}) copy-start(s32[1,150,2]{1,2,0:T(2,128)} %param.6) | copy-start | bytes 3604
  19.1 184.6 %all-to-all-start = ((bf16[150,4,4096]{2,0,1:T(8,128)(2,1)}), bf16[150,4,4096]{2,0,1:T(8,128)(2,1)}, u32[]{:S(2)}, u32[]{:S(2)}) async-start(bf16[150,4,4096]{2,0,1:T(8,128)(2,1)} %copy.23), calls=%async_computation | async-start | bytes 9961472 | tf_op jit(solution)/shard_map/all_to_all | solution.py:80
  145.5 56.3 %copy-start.6 = (s32[32]{0:T(128)S(1)}, s32[32]{0:T(128)}, u32[]{:S(2)}) copy-start(s32[32]{0:T(128)} %param.8) | copy-start | bytes 388
  247.6 52.7 %all-to-all-start.1 = ((f32[1,250,4096]{1,0,2:T(1,128)}), f32[1,250,4096]{1,0,2:T(1,128)}, u32[]{:S(2)}, u32[]{:S(2)}) async-start(f32[1,250,4096]{1,0,2:T(1,128)} %copy.24), calls=%async_computation.1 | async-start | bytes 8388608 | tf_op jit(solution)/shard_map/all_to_all | solution.py:90
  254.6 8.6 %copy-start.4 = (s32[4,250]{1,0:T(4,128)S(1)}, s32[4,250]{1,0:T(4,128)}, u32[]{:S(2)}) copy-start(s32[4,250]{1,0:T(4,128)} %param.7) | copy-start | bytes 12004
  310.4 6.9 %copy-start.1 = (f32[320,1024]{1,0:T(8,128)S(1)}, f32[320,1024]{1,0:T(8,128)}, u32[]{:S(2)}) copy-start(f32[320,1024]{1,0:T(8,128)} %convolution_add_fusion) | copy-start | bytes 3932164
  310.4 6.9 %copy-start.2 = (f32[320,1024]{1,0:T(8,128)S(1)}, f32[320,1024]{1,0:T(8,128)}, u32[]{:S(2)}) copy-start(f32[320,1024]{1,0:T(8,128)} %convolution_add_fusion.1) | copy-start | bytes 3932164
  310.4 6.9 %copy-start.3 = (f32[320,1024]{1,0:T(8,128)S(1)}, f32[320,1024]{1,0:T(8,128)}, u32[]{:S(2)}) copy-start(f32[320,1024]{1,0:T(8,128)} %convolution_add_fusion.2) | copy-start | bytes 3932164
  320.9 3.3 %copy-start = (f32[3,320,1024]{2,1,0:T(8,128)}, f32[3,320,1024]{2,1,0:T(8,128)S(1)}, u32[]{:S(2)}) copy-start(f32[3,320,1024]{2,1,0:T(8,128)S(1)} %pad_maximum_fusion) | copy-start | bytes 11796484
where the time goes:
time: 329 us; the launch traced here: 324 us
  blocking collectives  132 us (40%)
  other arithmetic  66.8 us (20%)
  local copies, waits for them, and re-layouts  46.8 us (14%)
  matrix products  36.4 us (11%)
  waiting for transfers between devices  27.3 us (8%)
  starting transfers between devices  11.5 us (3%)
  between operations  3.84 us (1%)
    all_gather x1, blocking collectives, shards(): pair_all = lax.all_gather(pair_rows, 'ifg', axis=0, tiled=True)  118 us
    another operation x7, other arithmetic, inverse_normal(): factor = jnp.linalg.cholesky(normal)  34 us
    all_to_all x1, waiting for transfers between devices, shards(): lax.all_to_all(series[None], 'track', split_axis=2, concat_axis=0, tiled=...  27.3 us
    all_to_all x3, local copies, waits for them, and re-layouts, shards(): lax.all_to_all(phase_rows, 'ifg', split_axis=1, concat_axis=0, tiled=True)  24.4 us
    another operation x6, other arithmetic, inverse_normal(): jax.scipy.linalg.cho_solve((factor, True), jnp.eye(ndate, dtype=jnp.float...  20.3 us
    psum x1, blocking collectives, shards(): total = lax.psum(jnp.sum(series, axis=1), ('ifg', 'pix'))  13.6 us
    dot_general x6, matrix products, entry(): jnp.einsum('tc,tp->cp', seen, look[:, first] * look[:, second], precision...  12.6 us
    broadcast_in_dim x1, local copies, waits for them, and re-layouts, shards(): series[None]  10.2 us
  transfers between devices with their start and end apart: 2, of which 1 were waited for; matrix products, arithmetic and copies ran while one was open for 24% of the time, Pallas kernels for 0%

commit v1 on v0

--- a/solution.py
+++ b/solution.py
@@ -87,7 +87,12 @@
     series = jnp.dot(ninv, rhs, precision=HIGH)
     total = lax.psum(jnp.sum(series, axis=1), ("ifg", "pix"))
     series = series - (total / pixel_count)[:, None]
-    gathered = lax.all_to_all(series[None], "track", split_axis=2, concat_axis=0, tiled=True)
+    gathered = jnp.concatenate(
+        lax.all_to_all(
+            jnp.stack(jnp.split(series[None], lax.axis_size("track"), axis=2)), "track", 0, 0
+        ),
+        axis=0,
+    )
     return geometry(gathered, date_map, look_local, knots, n_epochs)
 
 

time: 329 us -> 312 us (0.948)
  local copies, waits for them, and re-layouts: 46.8 us -> 33.3 us
    broadcast_in_dim x1 -> x0, local copies, waits for them, and re-layouts: 10.2 us -> none  [shards(): series[None]]
    another operation x0 -> x2, local copies, waits for them, and re-layouts: none -> 6.7 us  [shards(): jnp.stack(jnp.split(series[None], lax.axis_size('track'), axis=2))]
    all_to_all x1 -> x0, local copies, waits for them, and re-layouts: 5.6 us -> none  [shards(): lax.all_to_all(series[None], 'track', split_axis=2, concat_axis=0, tiled=...]
    unnamed x16 -> x15, local copies, waits for them, and re-layouts: 4.58 us -> 0.15 us
  transfers between devices with their start and end apart: 2 -> 2, of which waited for: 1 -> 1; matrix products, arithmetic and copies ran while one was open for 24% -> 25% of each run, Pallas kernels for 0% -> 0%
where the time goes in v1:
time: 312 us; the launch traced here: 308 us
  blocking collectives  132 us (42%)
  other arithmetic  64.7 us (21%)
  matrix products  36.8 us (12%)
  local copies, waits for them, and re-layouts  33.3 us (11%)
  waiting for transfers between devices  26.1 us (8%)
  starting transfers between devices  11.5 us (4%)
  between operations  3.87 us (1%)
    all_gather x1, blocking collectives, shards(): pair_all = lax.all_gather(pair_rows, 'ifg', axis=0, tiled=True)  118 us
    another operation x7, other arithmetic, inverse_normal(): factor = jnp.linalg.cholesky(normal)  34 us
    all_to_all x1, waiting for transfers between devices, shards(): lax.all_to_all(jnp.stack(jnp.split(series[None], lax.axis_size('track'),...  26.1 us
    all_to_all x3, local copies, waits for them, and re-layouts, shards(): lax.all_to_all(phase_rows, 'ifg', split_axis=1, concat_axis=0, tiled=True)  24.4 us
    another operation x6, other arithmetic, inverse_normal(): jax.scipy.linalg.cho_solve((factor, True), jnp.eye(ndate, dtype=jnp.float...  20 us
    psum x1, blocking collectives, shards(): total = lax.psum(jnp.sum(series, axis=1), ('ifg', 'pix'))  13.6 us
    dot_general x6, matrix products, entry(): jnp.einsum('tc,tp->cp', seen, look[:, first] * look[:, second], precision...  12.8 us
    dot_general x1, matrix products, geometry(): resampled = jnp.einsum('tcd,tdp->tcp', onehot, series, precision=HIGH)  7.12 us
  transfers between devices with their start and end apart: 2, of which 1 were waited for; matrix products, arithmetic and copies ran while one was open for 25% of the time, Pallas kernels for 0%

profile of v1, /device:TPU:0, one launch (start us, length us, event | category | flops | bytes accessed | tf_op | source)
XLA Modules:
  0.0 308.0 jit_solution(17866302643728049910)
XLA Ops:
  0.6 11.1 %all_to_all.17 = bf16[150,4,4096]{2,1,0:T(4,128)(2,1)} reshape(bf16[1,150,16384]{2,1,0:T(8,128)(2,1)} %param.5) | data formatting | bytes 9830400 | tf_op jit(solution)/shard_map/all_to_all | solution.py:80
  11.7 7.3 %copy.19 = bf16[150,4,4096]{2,0,1:T(8,128)(2,1)} copy(bf16[150,4,4096]{2,1,0:T(4,128)(2,1)} %all_to_all.17) | data formatting | bytes 9830400 | tf_op jit(solution)/shard_map/all_to_all | solution.py:80
  19.1 6.5 %all-to-all-start = ((bf16[150,4,4096]{2,0,1:T(8,128)(2,1)}), bf16[150,4,4096]{2,0,1:T(8,128)(2,1)}, u32[]{:S(2)}, u32[]{:S(2)}) async-start(bf16[150,4,4096]{2,0,1:T(8,128)(2,1)} %copy.19), calls=%async_computation | async-start | bytes 9961472 | tf_op jit(solution)/shard_map/all_to_all | solution.py:80
  25.7 118.2 %all-gather = s32[1,600,2]{2,0,1:T(1,128)S(1)} all-gather(s32[1,150,2]{2,0,1:T(1,128)S(1)} %copy.17), channel_id=2, replica_groups=mesh['track'=4,'ifg'=4,'pix'=2] {'ifg'}, dimensions={1}, use_global_device_ids=true | all-gather | bytes 6000 | tf_op jit(solution)/shard_map/all_gather | solution.py:81
  144.3 1.0 fusion.4
  145.5 11.7 %cholesky.63 = f32[128,128]{1,0:T(8,128)S(1)} custom-call(f32[128,128]{1,0:T(8,128)S(1)} %cholesky.156), custom_call_target="Cholesky" | custom-call | tf_op jit(solution)/shard_map/jit(cholesky)/cholesky | solution.py:22
  157.3 9.8 %custom-call.28 = f32[1,128,128]{1,2,0:T(8,128)S(1)} custom-call(f32[1,128,128]{2,1,0:T(8,128)S(1)} %get-tuple-element.44), custom_call_target="InvertDiagBlocksLowerTriangular" | custom-call | tf_op jit(solution)/shard_map/jit(cholesky)/cholesky | solution.py:22
  167.6 11.2 %cholesky.133 = f32[122,122]{1,0:T(8,128)S(1)} custom-call(f32[122,122]{1,0:T(8,128)S(1)} %convolution_subtract_fusion.2), custom_call_target="Cholesky" | custom-call | tf_op jit(solution)/shard_map/jit(cholesky)/cholesky | solution.py:22
  178.8 0.6 compare_reduce_fusion.1
  179.5 0.6 compare_reduce_fusion.2
  181.6 19.8 %custom-call.29 = f32[2,128,128]{1,2,0:T(8,128)S(1)} custom-call(f32[2,128,128]{2,1,0:T(8,128)S(1)} %pad_maximum_fusion.2), custom_call_target="InvertDiagBlocksLowerTriangular" | custom-call | tf_op jit(solution)/shard_map/jit(_cho_solve)/triangular_solve | solution.py:23
  203.3 6.0 %all_to_all.20 = bf16[600,4096]{1,0:T(8,128)(2,1)} reshape(bf16[4,150,4096]{2,1,0:T(8,128)(2,1)} %bitcast.11) | data formatting | bytes 9830400 | tf_op jit(solution)/shard_map/all_to_all | solution.py:80
  209.2 4.2 %fusion.6 = f32[250,4096]{1,0:T(8,128)S(1)} fusion(bf16[600,4096]{1,0:T(8,128)(2,1)} %all_to_all.20, s32[600]{0:T(1024)S(1)} %get-tuple-element.26, s32[600]{0:T(1024)S(1)} %get-tuple-element.25), kind=kOutput, calls=%fused_computation.37 | convolution fusion | flops 1229699968 | bytes 9016000 | tf_op jit(solution)/shard_map/dot_general | solution.py:84
  213.5 5.3 %fusion.49 = (f32[250]{0:T(256)S(1)}, f32[250,4096]{1,0:T(8,128)}) fusion(f32[250,4096]{1,0:T(8,128)S(1)} %fusion.6, f32[122,250]{1,0:T(8,128)S(1)} %fusion.27, f32[128,250]{1,0:T(8,128)S(1)} %fusion.26), kind=kOutput, calls=%fused_computation.119 | convolution fusion | flops 3073086208 | bytes 8443000 | tf_op jit(solution)/shard_map/dot_general | solution.py:87
  218.7 13.6 %psum.7 = f32[250]{0:T(256)S(1)} all-reduce(f32[250]{0:T(256)S(1)} %get-tuple-element.53), channel_id=1, replica_groups=mesh['track'=4,'ifg'=4,'pix'=2] {'ifg','pix'}, use_global_device_ids=true, to_apply=%region_6.7 | all-reduce | flops 250 | bytes 2000 | tf_op jit(solution)/shard_map/psum | solution.py:88
  232.3 2.6 subtract_bitcast_fusion
  235.9 6.1 %copy.20 = f32[4,1,250,1024]{3,1,2,0:T(1,128)} copy(f32[4,1,250,1024]{3,2,1,0:T(8,128)S(1)} %pad_maximum_fusion) | data formatting | bytes 8192000 | tf_op jit(solution)/shard_map/stack | solution.py:92
  242.0 5.0 %all-to-all-start.1 = ((f32[4,1,250,1024]{3,1,2,0:T(1,128)}), f32[4,1,250,1024]{3,1,2,0:T(1,128)}, u32[]{:S(2)}, u32[]{:S(2)}) async-start(f32[4,1,250,1024]{3,1,2,0:T(1,128)} %copy.20), calls=%async_computation.1 | async-start | bytes 8192000 | tf_op jit(solution)/shard_map/all_to_all | solution.py:91
  249.5 2.9 cholesky.147
  252.5 0.6 compare_reduce_fusion
  253.1 0.7 fusion.31
  253.8 2.4 custom-call.30
  256.2 0.8 dynamic-slice_bitcast_fusion.2
  257.8 2.3 convolution_add_fusion
  260.2 2.4 convolution_add_fusion.1
  262.6 2.3 convolution_add_fusion.2
  264.9 1.2 fusion.36
  266.1 1.3 fusion.38
  267.4 26.1 %all-to-all-done.1 = f32[4,1,250,1024]{3,1,2,0:T(1,128)} async-done(((f32[4,1,250,1024]{3,1,2,0:T(1,128)}), f32[4,1,250,1024]{3,1,2,0:T(1,128)}, u32[]{:S(2)}, u32[]{:S(2)}) %all-to-all-start.1) | async-done | bytes 4096032 | tf_op jit(solution)/shard_map/all_to_all | solution.py:91
  293.5 7.1 %multiply_reduce_fusion.2 = (f32[320,1024]{1,0:T(8,128)S(1)}, f32[320,1024]{1,0:T(8,128)S(1)}, f32[320,1024]{1,0:T(8,128)S(1)}) fusion(f32[4,1024]{1,0:T(4,128)S(1)} %get-tuple-element.40, f32[4,1024]{1,0:T(4,128)S(1)} %get-tuple-element.39, f32[4,1024]{1,0:T(4,128)S(1)} %get-tuple-element.38, f32[4,1,250,1024]{3,1,2,0:T(1,128)} %all-to-all-done.1, ...), kind=kOutput, calls=%fused_computation.2 | convolution fusion | flops 3939361280 | bytes 8081312 | tf_op jit(solution)/shard_map/tcd,tdp->tcp/dot_general | solution.py:40
  300.6 3.3 %divide_bitcast_fusion.2 = (f32[1,320,1024]{2,1,0:T(8,128)S(1)}, f32[1,320,1024]{2,1,0:T(8,128)S(1)}, f32[1,320,1024]{2,1,0:T(8,128)S(1)}) fusion(f32[320,1024]{1,0:T(8,128)S(1)} %get-tuple-element.23, f32[320,1024]{1,0:T(8,128)S(1)} %get-tuple-element.24, f32[320,1024]{1,0:T(8,128)S(1)} %get-tuple-element.22, f32[320,1024]{1,0:T(8,128)S(1)} %copy-done.3, ...), kind=kOutput, calls=%fused_computation.15 | convolution fusion | flops 29167616 | bytes 14455808 | tf_op jit(solution)/shard_map/tc,tp->cp/dot_general | solution.py:43
  304.5 3.3 %convolution_bitcast_fusion = f32[3,32,1024]{2,1,0:T(8,128)} fusion(f32[3,320,1024]{2,1,0:T(8,128)S(1)} %pad_maximum_fusion.1, f32[32,320,1]{1,0,2:T(8,128)S(1)} %convolution_bitcast_fusion.1), kind=kOutput, calls=%fused_computation.22 | convolution fusion | flops 377487360 | bytes 4366336 | tf_op jit(solution)/shard_map/kc,icp->ikp/dot_general | solution.py:66
  (53 shorter events, 6.6 us)
Async XLA Ops:
  19.1 6.5 %copy-start.5 = (s32[1,150,2]{1,2,0:T(2,128)S(1)}, s32[1,150,2]{1,2,0:T(2,128)}, u32[]{:S(2)}) copy-start(s32[1,150,2]{1,2,0:T(2,128)} %param.6) | copy-start | bytes 3604
  19.1 184.2 %all-to-all-start = ((bf16[150,4,4096]{2,0,1:T(8,128)(2,1)}), bf16[150,4,4096]{2,0,1:T(8,128)(2,1)}, u32[]{:S(2)}, u32[]{:S(2)}) async-start(bf16[150,4,4096]{2,0,1:T(8,128)(2,1)} %copy.19), calls=%async_computation | async-start | bytes 9961472 | tf_op jit(solution)/shard_map/all_to_all | solution.py:80
  145.5 55.9 %copy-start.6 = (s32[32]{0:T(128)S(1)}, s32[32]{0:T(128)}, u32[]{:S(2)}) copy-start(s32[32]{0:T(128)} %param.8) | copy-start | bytes 388
  242.0 51.5 %all-to-all-start.1 = ((f32[4,1,250,1024]{3,1,2,0:T(1,128)}), f32[4,1,250,1024]{3,1,2,0:T(1,128)}, u32[]{:S(2)}, u32[]{:S(2)}) async-start(f32[4,1,250,1024]{3,1,2,0:T(1,128)} %copy.20), calls=%async_computation.1 | async-start | bytes 8192000 | tf_op jit(solution)/shard_map/all_to_all | solution.py:91
  249.0 8.6 %copy-start.4 = (s32[4,250]{1,0:T(4,128)S(1)}, s32[4,250]{1,0:T(4,128)}, u32[]{:S(2)}) copy-start(s32[4,250]{1,0:T(4,128)} %param.7) | copy-start | bytes 12004
  293.5 7.1 %copy-start.1 = (f32[320,1024]{1,0:T(8,128)S(1)}, f32[320,1024]{1,0:T(8,128)}, u32[]{:S(2)}) copy-start(f32[320,1024]{1,0:T(8,128)} %convolution_add_fusion) | copy-start | bytes 3932164
  293.5 7.1 %copy-start.2 = (f32[320,1024]{1,0:T(8,128)S(1)}, f32[320,1024]{1,0:T(8,128)}, u32[]{:S(2)}) copy-start(f32[320,1024]{1,0:T(8,128)} %convolution_add_fusion.1) | copy-start | bytes 3932164
  293.5 7.2 %copy-start.3 = (f32[320,1024]{1,0:T(8,128)S(1)}, f32[320,1024]{1,0:T(8,128)}, u32[]{:S(2)}) copy-start(f32[320,1024]{1,0:T(8,128)} %convolution_add_fusion.2) | copy-start | bytes 3932164
  304.4 3.3 %copy-start = (f32[3,320,1024]{2,1,0:T(8,128)}, f32[3,320,1024]{2,1,0:T(8,128)S(1)}, u32[]{:S(2)}) copy-start(f32[3,320,1024]{2,1,0:T(8,128)S(1)} %pad_maximum_fusion.1) | copy-start | bytes 11796484
